TPU v7x, 128 devices: a whole 4x4x4 slice. The times are simulated.
128 devices in a mesh: batch: 32 (over z, y, x_hi), mp: 4 (over x_lo, core).
Axes of the slice: x: 4 (x_hi: 2, x_lo: 2; x = x_hi * 2 + x_lo), y: 4, z: 4, core: 2. Of those that a mesh axis runs over, the one named last changes fastest.
Arguments:
- lookup_ids: int32 [64, 65536], P('batch'), may hold values from 0 to 8191
- table_feature: int32 [64], replicated, may hold values from 0 to 63, each once
- tables: bfloat16 [64, 8192, 128], P('batch'), may hold values from -6 to 6
- cross_down: bfloat16 [2, 8192, 512], P(None, 'mp'), may hold values from -0.0625 to 0.0625
- cross_up: bfloat16 [2, 512, 8192], P(None, None, 'mp'), may hold values from -0.25 to 0.25
- cross_bias: float32 [2, 8192], P(None, 'mp'), may hold values from -3 to 3
Outputs:
- crossed: bfloat16 [65536, 8192], P('batch', 'mp')
Inputs may be any that keep to these rules, and one draw needn't show every extreme that they name: `table_feature`: each number appears once.
All inputs are finite; a program needn't handle non-finite values.
Results may differ from a plain program's by a relative error of at most 0.015.
Values may be sent and summed in bfloat16 or wider, within the bound.
A program may use at most 128 MiB of HBM per device.

v0:
```python
import jax
import jax.numpy as jnp
from jax import lax
from jax.sharding import PartitionSpec as P


def in_blocks(x, dim, size):
    shape = x.shape
    parts = x.reshape(*shape[:dim], size, shape[dim] // size, *shape[dim + 1 :])
    return jnp.moveaxis(parts, dim, 0)


def laid_out(parts, dim):
    shape = list(parts.shape[1:])
    shape[dim] *= parts.shape[0]
    return jnp.moveaxis(parts, 0, dim).reshape(shape)


def one_exchange(x, axis, axes, splits, concats):
    sizes = [lax.axis_size(a) for a in axes]
    parts = in_blocks(x, splits[0], sizes[0])
    parts = jnp.moveaxis(in_blocks(parts, splits[1] + 1, sizes[1]), 0, 1)
    inside = parts.shape[2:]
    parts = parts.reshape(-1, *inside)
    parts = lax.all_to_all(parts, axis, split_axis=0, concat_axis=0, tiled=True)
    parts = laid_out(parts.reshape(*sizes, *inside), concats[0] + 1)
    return laid_out(parts, concats[1])


def sent_and_summed(x, axis, dim):
    size = lax.axis_size(axis)
    parts = lax.all_to_all(in_blocks(x, dim, size), axis, 0, 0, tiled=True)
    return jnp.sum(parts.astype(jnp.float32), axis=0)


def from_everyone(x, axis):
    size = lax.axis_size(axis)
    return lax.all_to_all(jnp.broadcast_to(x[None], (size, *x.shape)), axis, 0, 0, tiled=True)


def gathered_copies(x, axis, dim):
    return laid_out(from_everyone(x, axis), dim)


def per_device(lookup_ids, table_feature, tables, cross_down, cross_up, cross_bias):
    slots_local = tables.shape[0]
    feats = table_feature.shape[0]
    sources = lax.axis_size("batch")
    groups = lax.axis_size("mp")
    examples_local = lookup_ids.shape[1] // sources
    share = examples_local // groups
    start = lax.axis_index("mp") * share
    by_owner = lookup_ids.reshape(slots_local, sources, examples_local)
    wanted = lax.dynamic_slice_in_dim(by_owner, start, share, 2)
    looked = jnp.stack(
        [
            jnp.take(tables[slot], wanted[slot].reshape(sources * share), axis=0)
            for slot in range(slots_local)
        ],
        axis=1,
    )
    looked = looked.reshape(sources, share, slots_local, tables.shape[2])
    received = one_exchange(looked, ("batch", "mp"), ("batch", "mp"), (0, 3), (0, 1))
    emb_local = received.shape[3]
    unfolded = jnp.transpose(received, (1, 0, 2, 3)).reshape(examples_local, feats, emb_local)
    placing = (table_feature[:, None] == jnp.arange(feats, dtype=jnp.int32)[None, :]).astype(
        jnp.bfloat16
    )
    ordered = jnp.einsum("rse,sf->ref", unfolded, placing, preferred_element_type=jnp.float32)
    embedded = ordered.astype(jnp.bfloat16).reshape(examples_local, emb_local * feats)
    embedded_wide = embedded.astype(jnp.float32)
    state = embedded
    for layer in range(len(cross_down)):
        weight_down = cross_down[layer]
        current = state
        product = jnp.dot(current, weight_down, preferred_element_type=jnp.float32)
        mine = sent_and_summed(
            product.astype(jnp.bfloat16).astype(jnp.float32).astype(jnp.bfloat16), "mp", 0
        ).astype(jnp.bfloat16)
        low = gathered_copies(mine, "mp", 0)
        high = (
            jnp.dot(low, cross_up[layer], preferred_element_type=jnp.float32)
            + cross_bias[layer][None, :]
        )
        state = (embedded_wide * high + state.astype(jnp.float32)).astype(jnp.bfloat16)
    return state


def solution(mesh):
    return jax.shard_map(
        per_device,
        mesh=mesh,
        in_specs=(
            P("batch", None),
            P(),
            P("batch", None, None),
            P(None, "mp", None),
            P(None, None, "mp"),
            P(None, "mp"),
        ),
        out_specs=P("batch", "mp"),
        check_vma=False,
    )
```

profile of v0, /device:TPU:1, one launch (start us, length us, event | category | flops | bytes accessed | tf_op | source)
XLA Modules:
  0.0 462.9 jit_solution(5163655522445915869)
XLA Ops:
  0.0 1.3 copy.30
  1.5 3.8 slice_bitcast_fusion.1
  5.4 57.3 %gather_fusion = bf16[16384,128]{1,0:T(8,128)(2,1)} fusion(bf16[8192,128]{1,0:T(8,128)(2,1)} %get-tuple-element.6, s32[16384]{0:T(1024)S(1)} %fusion.16), kind=kCustom, calls=%fused_computation.clone | custom fusion | bytes 8454144 | tf_op jit(solution)/shard_map/jit(_take)/gather | solution.py:57
  62.7 11.5 %broadcast_select_fusion.1 = bf16[16384,128]{1,0:T(8,128)(2,1)} fusion(bf16[16384,128]{1,0:T(8,128)(2,1)} %gather_fusion, pred[16384]{0:T(1024)(128)(4,1)S(1)} %compare_and_fusion.1), kind=kLoop, calls=%fused_computation.12 | loop fusion | flops 2097152 | bytes 8404992 | tf_op jit(solution)/shard_map/jit(_take)/select_n | solution.py:57
  74.2 6.5 %copy.12 = bf16[16384,128]{0,1:T(8,128)(2,1)} copy(bf16[16384,128]{1,0:T(8,128)(2,1)} %broadcast_select_fusion.1) | data formatting | bytes 8388608 | tf_op jit(solution)/shard_map/jit(_take)/select_n | solution.py:57
  80.7 5.9 %copy.22 = bf16[16,8,32,512]{3,2,1,0:T(8,128)(2,1)} copy(bf16[16,8,32,512]{3,1,2,0:T(8,128)(2,1)} %bitcast.71) | data formatting | bytes 8388608
  86.5 57.9 %gather_fusion.1 = bf16[16384,128]{1,0:T(8,128)(2,1)} fusion(bf16[8192,128]{1,0:T(8,128)(2,1)S(1)} %get-tuple-element.7, s32[16384]{0:T(1024)S(1)} %fusion.17), kind=kCustom, calls=%fused_computation.1.clone | custom fusion | bytes 8454144 | tf_op jit(solution)/shard_map/jit(_take)/gather | solution.py:57
  144.4 11.5 %broadcast_select_fusion = bf16[16384,128]{1,0:T(8,128)(2,1)} fusion(bf16[16384,128]{1,0:T(8,128)(2,1)} %gather_fusion.1, pred[16384]{0:T(1024)(128)(4,1)S(1)} %compare_and_fusion), kind=kLoop, calls=%fused_computation.11 | loop fusion | flops 2097152 | bytes 8404992 | tf_op jit(solution)/shard_map/jit(_take)/select_n | solution.py:57
  155.9 6.5 %copy.13 = bf16[16384,128]{0,1:T(8,128)(2,1)} copy(bf16[16384,128]{1,0:T(8,128)(2,1)} %broadcast_select_fusion) | data formatting | bytes 8388608 | tf_op jit(solution)/shard_map/jit(_take)/select_n | solution.py:57
  162.4 0.0 copy-start.1
  162.4 6.0 %copy.24 = bf16[16,8,32,512]{3,2,1,0:T(8,128)(2,1)} copy(bf16[16,8,32,512]{3,1,2,0:T(8,128)(2,1)} %bitcast.72) | data formatting | bytes 8388608
  168.5 0.0 copy-done.1
  168.5 6.3 %maximum_bitcast_fusion = bf16[32,4,1,512,2,32]{3,0,5,1,4,2:T(8,128)(2,1)} fusion(bf16[32,1,512,1,4,32]{2,0,5,4,3,1:T(8,128)(2,1)} %bitcast.74, bf16[32,1,512,1,4,32]{2,0,5,4,3,1:T(8,128)(2,1)S(1)} %bitcast.73), kind=kLoop, calls=%fused_computation.7 | loop fusion | flops 4194304 | bytes 16777216 | tf_op jit(solution)/shard_map/transpose;transpose | solution.py:22
  174.8 11.3 %copy.14 = bf16[32,4,1,512,2,32]{3,5,4,2,1,0:T(8,128)(2,1)} copy(bf16[32,4,1,512,2,32]{3,0,5,1,4,2:T(8,128)(2,1)} %maximum_bitcast_fusion) | data formatting | bytes 16777216 | tf_op jit(solution)/shard_map/transpose;transpose | solution.py:22
  186.2 109.5 %all_to_all.25 = bf16[128,1,512,2,32]{2,4,3,1,0:T(8,128)(2,1)} all-to-all(bf16[128,1,512,2,32]{2,4,3,1,0:T(8,128)(2,1)} %bitcast.69), channel_id=1, replica_groups=mesh['batch'=32,'mp'=4] {'batch','mp'}, dimensions={0} | all-to-all | bytes 16777216 | tf_op jit(solution)/shard_map/all_to_all | solution.py:25
  295.6 0.0 copy-start.3
  295.6 8.1 %copy.19 = bf16[32,4,2,4,8,512]{5,4,1,3,2,0:T(8,128)(2,1)} copy(bf16[32,4,2,4,8,512]{5,4,3,2,1,0:T(8,128)(2,1)} %bitcast.70) | data formatting | bytes 16777216 | tf_op jit(solution)/shard_map/reshape | solution.py:16
  303.7 0.0 copy-done.3
  303.8 10.1 %fusion.5 = bf16[2048,32,64]{0,2,1:T(8,128)(2,1)S(1)} fusion(bf16[2048,64,32]{0,2,1:T(8,128)(2,1)} %bitcast.68, s32[64]{0:T(128)S(1)} %copy-done.3), kind=kOutput, calls=%fused_computation.10 | convolution fusion | flops 541069312 | bytes 16777472 | tf_op jit(solution)/shard_map/rse,sf->ref/dot_general | solution.py:69
  313.8 0.0 copy-start
  313.8 7.9 %convolution_convert_fusion.1 = bf16[2048,512]{1,0:T(8,128)(2,1)S(1)} fusion(bf16[2048,2048]{0,1:T(8,128)(2,1)S(1)} %bitcast.66, bf16[2,2048,512]{2,1,0:T(8,128)(2,1)} %param.11), kind=kOutput, calls=%fused_computation.14 | convolution fusion | flops 4296015872 | bytes 12582912 | tf_op jit(solution)/shard_map/dot_general | solution.py:76
  321.8 0.0 copy-done
  321.8 28.1 %all_to_all.26 = bf16[4,512,512]{2,1,0:T(8,128)(2,1)S(1)} all-to-all(bf16[4,512,512]{2,1,0:T(8,128)(2,1)S(1)} %bitcast.77), channel_id=1, replica_groups=mesh['batch'=32,'mp'=4] {'mp'}, dimensions={0} | all-to-all | bytes 4194304 | tf_op jit(solution)/shard_map/all_to_all | solution.py:32
  349.9 0.0 copy-start.2
  349.9 0.6 reduce_sum.24
  350.5 1.5 broadcast_in_dim.13
  352.0 4.6 all-to-all-start.2
  356.6 0.0 copy-done.2
  356.7 12.4 %copy.17 = bf16[2048,2048]{1,0:T(8,128)(2,1)} copy(bf16[2048,2048]{0,1:T(8,128)(2,1)} %bitcast.67) | data formatting | bytes 16777216 | tf_op jit(solution)/shard_map/reshape | solution.py:70
  369.1 12.3 %all-to-all-done.2 = bf16[4,512,512]{2,1,0:T(8,128)(2,1)S(1)} async-done(((bf16[4,512,512]{2,1,0:T(8,128)(2,1)}), bf16[4,512,512]{2,1,0:T(8,128)(2,1)S(1)}, u32[]{:S(2)}, u32[]{:S(2)}) %all-to-all-start.2) | async-done | bytes 2097184 | tf_op jit(solution)/shard_map/all_to_all | solution.py:38
  381.3 0.0 copy-start.4
  381.3 8.1 %fusion.2 = bf16[2048,2048]{1,0:T(8,128)(2,1)S(1)} fusion(bf16[2048,2048]{1,0:T(8,128)(2,1)} %copy.17, f32[2048]{0:T(1024)S(1)} %bitcast.86, bf16[2048,512]{1,0:T(8,128)(2,1)S(1)} %bitcast.75, bf16[2,512,2048]{2,1,0:T(8,128)(2,1)} %param.12), kind=kOutput, calls=%fused_computation.6 | convolution fusion | flops 4315938816 | bytes 20979712 | tf_op jit(solution)/shard_map/dot_general | solution.py:82
  389.4 0.0 copy-done.4
  389.4 0.0 copy-start.6
  389.5 4.9 %convolution_convert_fusion = bf16[2048,512]{1,0:T(8,128)(2,1)S(1)} fusion(bf16[2048,2048]{1,0:T(8,128)(2,1)S(1)} %fusion.2, bf16[2,2048,512]{2,1,0:T(8,128)(2,1)S(1)} %copy-done.4), kind=kOutput, calls=%fused_computation.13 | convolution fusion | flops 4296015872 | bytes 12582912 | tf_op jit(solution)/shard_map/dot_general | solution.py:76
  394.4 0.0 copy-done.6
  394.4 28.1 %all_to_all.27 = bf16[4,512,512]{2,1,0:T(8,128)(2,1)S(1)} all-to-all(bf16[4,512,512]{2,1,0:T(8,128)(2,1)S(1)} %bitcast.78), channel_id=1, replica_groups=mesh['batch'=32,'mp'=4] {'mp'}, dimensions={0} | all-to-all | bytes 4194304 | tf_op jit(solution)/shard_map/all_to_all | solution.py:32
  422.5 0.6 reduce_sum.25
  423.1 0.0 copy-start.5
  423.1 0.2 broadcast_in_dim.14
  423.3 28.4 %all_to_all.28 = bf16[4,512,512]{2,1,0:T(8,128)(2,1)S(1)} all-to-all(bf16[4,512,512]{2,1,0:T(8,128)(2,1)S(1)} %broadcast_in_dim.14), channel_id=1, replica_groups=mesh['batch'=32,'mp'=4] {'mp'}, dimensions={0} | all-to-all | bytes 4194304 | tf_op jit(solution)/shard_map/all_to_all | solution.py:38
  451.7 0.0 copy-done.5
  451.7 11.2 %fusion.1 = bf16[2048,2048]{1,0:T(8,128)(2,1)} fusion(bf16[2048,2048]{1,0:T(8,128)(2,1)} %copy.17, bf16[2048,2048]{1,0:T(8,128)(2,1)} %copy-done.6, f32[2048]{0:T(1024)S(1)} %bitcast.85, bf16[2048,512]{1,0:T(8,128)(2,1)S(1)} %bitcast.76, bf16[2,512,2048]{2,1,0:T(8,128)(2,1)S(1)} %copy-done.5), kind=kOutput, calls=%fused_computation.5 | convolution fusion | flops 4320133120 | bytes 29368320 | tf_op jit(solution)/shard_map/dot_general | solution.py:82
  (8 shorter events, 0.2 us)
Async XLA Ops:
  162.4 6.1 %copy-start.1 = (bf16[16,8,32,512]{3,2,1,0:T(8,128)(2,1)S(1)}, bf16[16,8,32,512]{3,2,1,0:T(8,128)(2,1)}, u32[]{:S(2)}) copy-start(bf16[16,8,32,512]{3,2,1,0:T(8,128)(2,1)} %copy.22) | copy-start | bytes 12582916
  295.6 8.1 %copy-start.3 = (s32[64]{0:T(128)S(1)}, s32[64]{0:T(128)}, u32[]{:S(2)}) copy-start(s32[64]{0:T(128)} %param.9) | copy-start | bytes 772
  313.8 8.0 %copy-start = (bf16[2048,32,64]{0,2,1:T(8,128)(2,1)}, bf16[2048,32,64]{0,2,1:T(8,128)(2,1)S(1)}, u32[]{:S(2)}) copy-start(bf16[2048,32,64]{0,2,1:T(8,128)(2,1)S(1)} %fusion.5) | copy-start | bytes 25165828
  349.9 6.8 %copy-start.2 = (f32[2,2048]{1,0:T(2,128)S(1)}, f32[2,2048]{1,0:T(2,128)}, u32[]{:S(2)}) copy-start(f32[2,2048]{1,0:T(2,128)} %param.13) | copy-start | bytes 49156
  352.0 29.3 %all-to-all-start.2 = ((bf16[4,512,512]{2,1,0:T(8,128)(2,1)}), bf16[4,512,512]{2,1,0:T(8,128)(2,1)S(1)}, u32[]{:S(2)}, u32[]{:S(2)}) async-start(bf16[4,512,512]{2,1,0:T(8,128)(2,1)} %broadcast_in_dim.13), calls=%async_computation.2 | async-start | bytes 4194304 | tf_op jit(solution)/shard_map/all_to_all | solution.py:38
  381.3 8.1 %copy-start.4 = (bf16[2,2048,512]{2,1,0:T(8,128)(2,1)S(1)}, bf16[2,2048,512]{2,1,0:T(8,128)(2,1)}, u32[]{:S(2)}) copy-start(bf16[2,2048,512]{2,1,0:T(8,128)(2,1)} %param.11) | copy-start | bytes 12582916
  389.4 5.0 %copy-start.6 = (bf16[2048,2048]{1,0:T(8,128)(2,1)}, bf16[2048,2048]{1,0:T(8,128)(2,1)S(1)}, u32[]{:S(2)}) copy-start(bf16[2048,2048]{1,0:T(8,128)(2,1)S(1)} %fusion.2) | copy-start | bytes 25165828
  423.1 28.6 %copy-start.5 = (bf16[2,512,2048]{2,1,0:T(8,128)(2,1)S(1)}, bf16[2,512,2048]{2,1,0:T(8,128)(2,1)}, u32[]{:S(2)}) copy-start(bf16[2,512,2048]{2,1,0:T(8,128)(2,1)} %param.12) | copy-start | bytes 12582916
where the time goes:
time: 465 us; the launch traced here: 463 us
  blocking collectives  194 us (42%)
  local copies, waits for them, and re-layouts  179 us (38%)
  matrix products  42.3 us (9%)
  other arithmetic  30.7 us (7%)
  waiting for transfers between devices  12.3 us (3%)
    gather x2, local copies, waits for them, and re-layouts, per_device(): jnp.take(tables[slot], wanted[slot].reshape(sources * share), axis=0)  115 us
    all_to_all x1, blocking collectives, one_exchange(): parts = lax.all_to_all(parts, axis, split_axis=0, concat_axis=0, tiled=True)  109 us
    all_to_all x2, blocking collectives, sent_and_summed(): parts = lax.all_to_all(in_blocks(x, dim, size), axis, 0, 0, tiled=True)  56.1 us
    all_to_all x1, blocking collectives, from_everyone(): lax.all_to_all(jnp.broadcast_to(x[None], (size, *x.shape)), axis, 0, 0, t...  28.4 us
    select_n x2, other arithmetic, per_device(): jnp.take(tables[slot], wanted[slot].reshape(sources * share), axis=0)  23 us
    dot_general x2, matrix products, per_device(): jnp.dot(low, cross_up[layer], preferred_element_type=jnp.float32)  19.3 us
    unnamed x20, local copies, waits for them, and re-layouts  13.4 us
    select_n x2, local copies, waits for them, and re-layouts, per_device(): jnp.take(tables[slot], wanted[slot].reshape(sources * share), axis=0)  13 us
  transfers between devices with their start and end apart: 1, of which 1 were waited for; matrix products, arithmetic and copies ran while one was open for 3% of the time, Pallas kernels for 0%

commit v1 on v0

v1 whole, which is shorter than its diff:
```python
import functools

import jax
import jax.numpy as jnp
from jax import lax
from jax.experimental import pallas as pl
from jax.experimental.pallas import tpu as pltpu
from jax.sharding import PartitionSpec as P

MESH = pl.DeviceIdType.MESH
UNROLL = 64
F32 = jnp.float32
BF16 = jnp.bfloat16


def kernel(
    sizes,
    ids,
    tables,
    placing,
    downs,
    ups,
    bias,
    out,
    table,
    rows,
    pick,
    message,
    landed,
    emb,
    state,
    weight_down,
    weight_up,
    part,
    near,
    summed,
    far,
    low,
    send_sem,
    recv_sem,
    load_sem,
    out_sem,
    hop_send,
    hop_recv,
):
    groups, members, chunks, share, slot_rows = sizes
    peers = groups * members
    b = lax.axis_index("batch")
    m = lax.axis_index("mp")
    me = b * members + m
    core = lax.rem(m, 2)
    partner = {"mp": m + 1 - 2 * core}
    across = {"mp": lax.rem(m + 2, 4)}
    width = emb.shape[2]
    rank = low.shape[2]
    tile = members * share
    half = tile // 2
    mine = pl.multiple_of(core * half, half)
    theirs = pl.multiple_of((1 - core) * half, half)

    barrier = pltpu.get_barrier_semaphore()

    def greet(i, _):
        other = lax.rem(me + i, peers)
        pl.semaphore_signal(
            barrier,
            inc=1,
            device_id={"batch": other // members, "mp": lax.rem(other, members)},
            device_id_type=MESH,
        )
        return 0

    held = tables.shape[0]
    first = chunks - held
    load_table = pltpu.make_async_copy(tables, message.at[pl.ds(first, held)], load_sem.at[0])
    load_table.start()
    load_down = pltpu.make_async_copy(downs, weight_down, load_sem.at[1])
    load_down.start()
    load_up = pltpu.make_async_copy(ups, weight_up, load_sem.at[2])
    load_up.start()
    lax.fori_loop(1, peers, greet, 0)

    row = lax.broadcasted_iota(jnp.int32, (256, 256), 0)
    col = lax.broadcasted_iota(jnp.int32, (256, 256), 1)
    wanted = ((row // 4) % 2) * 128 + (row // 8) * 4 + row % 4
    pick[...] = (wanted == col).astype(BF16)

    load_table.wait()

    block_rows = message.shape[2]
    for slot in range(held):

        def widen(i, _):
            at = pl.multiple_of(slot * slot_rows + i * block_rows, block_rows)
            table[pl.ds(at, block_rows), :] = message[first + slot, i].astype(F32)
            return 0

        lax.fori_loop(0, slot_rows // block_rows, widen, 0)

    def look(chunk, dest):
        def group(g, _):
            for u in range(UNROLL):
                for slot in range(2):
                    index = ids[(dest * chunks + chunk) * (2 * share) + slot * share + g * UNROLL + u]
                    rows[g, u : u + 1, slot * 128 : (slot + 1) * 128] = table[
                        pl.ds(index + slot * slot_rows, 1), :
                    ]
            return 0

        lax.fori_loop(0, share // UNROLL, group, 0)
        looked = rows[...].reshape(share, 256).astype(BF16)
        return (
            lax.dot_general(
                pick[...], looked, (((1,), (1,)), ((), ())), preferred_element_type=F32
            )
            .astype(BF16)
            .reshape(members, 64, share)
        )

    def send(chunk, dest, member):
        pltpu.make_async_remote_copy(
            src_ref=message.at[chunk, dest * members + member],
            dst_ref=landed.at[chunk, me],
            send_sem=send_sem.at[chunk],
            recv_sem=recv_sem.at[chunk],
            device_id={"batch": dest, "mp": member},
            device_id_type=MESH,
        ).start()

    def chunk_out(chunk, _):
        def one(i, _):
            dest = lax.rem(b + i, groups)
            message[chunk, pl.ds(dest * members, members)] = look(chunk, dest)

            @pl.when(jnp.logical_and(chunk == 0, i == 1))
            def _():
                pl.semaphore_wait(barrier, peers - 1)

            for k in range(members):
                send(chunk, dest, lax.rem(m + k, members))
            return 0

        lax.fori_loop(1, groups, one, 0)
        message[chunk, pl.ds(b * members, members)] = look(chunk, b)
        landed[chunk, me] = message[chunk, me]
        for k in range(1, members):
            send(chunk, b, lax.rem(m + k, members))
        return 0

    lax.fori_loop(0, chunks, chunk_out, 0)
    load_down.wait()
    load_up.wait()

    def hop(kind, t, src, dst, device):
        return pltpu.make_async_remote_copy(
            src_ref=src,
            dst_ref=dst,
            send_sem=hop_send.at[kind, t],
            recv_sem=hop_recv.at[kind, t],
            device_id=device,
            device_id_type=MESH,
        )

    def hop_near(layer, t):
        return hop(3 * layer, t, part.at[t, 1], near.at[t], partner)

    def hop_far(layer, t):
        return hop(3 * layer + 1, t, summed.at[t], far.at[layer, t], across)

    def hop_low(layer, t):
        there = low.at[t, pl.ds(mine, half)]
        return hop(3 * layer + 2, t, there, there, partner)

    def project(layer, t, source):
        for which, at in ((1, theirs), (0, mine)):
            product = jnp.dot(
                source[t, pl.ds(at, half), :], weight_down[layer], preferred_element_type=F32
            )
            part[t, which] = product.astype(BF16)
            if which == 1:
                hop_near(layer, t).start()

    def add_near(layer, t):
        hop_near(layer, t).wait()
        summed[t] = (part[t, 0].astype(F32) + near[t].astype(F32)).astype(BF16)
        hop_far(layer, t).start()

    def add_far(layer, t):
        hop_far(layer, t).wait()
        low[t, pl.ds(mine, half), :] = (
            summed[t].astype(F32) + far[layer, t].astype(F32)
        ).astype(BF16)
        hop_low(layer, t).start()

    def expand(layer, t, before):
        hop_low(layer, t).wait()

        def block(i, _):
            at = pl.ds(pl.multiple_of(i * 128, 128), 128)
            high = (
                jnp.dot(
                    low[t, at, :], weight_up[layer], preferred_element_type=F32
                )
                + bias[layer : layer + 1, :]
            )
            state[t, at, :] = (
                emb[t, at, :].astype(F32) * high + before[t, at, :].astype(F32)
            ).astype(BF16)
            return 0

        lax.fori_loop(0, tile // 128, block, 0)

    def place(t):
        pltpu.make_async_copy(
            message.at[t, pl.ds(0, peers - 1)], landed.at[t, pl.ds(0, peers - 1)], recv_sem.at[t]
        ).wait()

        def landed_of(t, i, hi):
            return jnp.concatenate(
                [landed[t, g * members + i, hi * 8 : (hi + 1) * 8, :] for g in range(groups)], axis=0
            )

        def member_rows(i, _):
            for hi in range(8):
                block = lax.dot_general(
                    landed_of(t, i, hi), placing[...], (((0,), (0,)), ((), ())), preferred_element_type=F32
                )
                emb[t, pl.ds(pl.multiple_of(i * share, share), share), hi * 256 : (hi + 1) * 256] = (
                    block.astype(BF16)
                )
            return 0

        lax.fori_loop(0, members, member_rows, 0)

    def store(t):
        return pltpu.make_async_copy(
            state.at[t], out.at[pl.ds(pl.multiple_of(t * tile, tile), tile)], out_sem.at[t]
        )

    def step(i, _):
        @pl.when(i >= 2)
        def _():
            expand(1, i - 2, state)
            store(i - 2).start()

        @pl.when(jnp.logical_and(i >= 1, i <= chunks))
        def _():
            expand(0, i - 1, emb)
            project(1, i - 1, state)

        @pl.when(i < chunks)
        def _():
            place(i)
            project(0, i, emb)

        @pl.when(jnp.logical_and(i >= 1, i <= chunks))
        def _():
            add_near(1, i - 1)

        @pl.when(i < chunks)
        def _():
            add_near(0, i)

        @pl.when(jnp.logical_and(i >= 1, i <= chunks))
        def _():
            add_far(1, i - 1)

        @pl.when(i < chunks)
        def _():
            add_far(0, i)

        return 0

    lax.fori_loop(0, chunks + 2, step, 0)

    def finish(t, _):
        store(t).wait()
        pltpu.make_async_copy(
            message.at[t, pl.ds(0, peers - 1)], landed.at[t, pl.ds(0, peers - 1)], send_sem.at[t]
        ).wait()
        return 0

    lax.fori_loop(0, chunks, finish, 0)


def per_device(lookup_ids, table_feature, tables, cross_down, cross_up, cross_bias):
    slots_local, slot_rows, emb_dim = tables.shape
    feats = table_feature.shape[0]
    groups = lax.axis_size("batch")
    members = lax.axis_size("mp")
    layers, width, rank = cross_down.shape
    examples = lookup_ids.shape[1] // groups
    chunks = 4
    share = examples // (chunks * members)
    tile = members * share
    mine = lookup_ids.reshape(slots_local, groups, chunks, members, share)
    mine = lax.dynamic_index_in_dim(mine, lax.axis_index("mp"), 3, keepdims=False)
    ids = jnp.transpose(mine, (1, 2, 0, 3)).reshape(-1)
    lane = jnp.arange(4 * feats, dtype=jnp.int32)
    placing = jnp.logical_and(
        (lane % 4)[:, None] == (lane // feats)[None, :],
        jnp.repeat(table_feature, 4)[:, None] == (lane % feats)[None, :],
    ).astype(BF16)
    peers = groups * members
    hbm = pl.BlockSpec(memory_space=pltpu.HBM)
    vmem = pl.BlockSpec(memory_space=pltpu.VMEM)
    dma = pltpu.SemaphoreType.DMA
    return pl.pallas_call(
        functools.partial(kernel, (groups, members, chunks, share, slot_rows)),
        out_shape=jax.ShapeDtypeStruct((examples, width), BF16),
        in_specs=[pl.BlockSpec(memory_space=pltpu.SMEM), hbm, vmem, hbm, hbm, vmem],
        out_specs=hbm,
        scratch_shapes=[
            pltpu.VMEM((slots_local * slot_rows, emb_dim), F32),
            pltpu.VMEM((share // UNROLL, UNROLL, slots_local * emb_dim), F32),
            pltpu.VMEM((256, 256), BF16),
            pltpu.VMEM((chunks, peers, 64, share), BF16),
            pltpu.VMEM((chunks, peers, 64, share), BF16),
            pltpu.VMEM((chunks, tile, width), BF16),
            pltpu.VMEM((chunks, tile, width), BF16),
            pltpu.VMEM((layers, width, rank), BF16),
            pltpu.VMEM((layers, rank, width), BF16),
            pltpu.VMEM((chunks, 2, tile // 2, rank), BF16),
            pltpu.VMEM((chunks, tile // 2, rank), BF16),
            pltpu.VMEM((chunks, tile // 2, rank), BF16),
            pltpu.VMEM((layers, chunks, tile // 2, rank), BF16),
            pltpu.VMEM((chunks, tile, rank), BF16),
            dma((chunks,)),
            dma((chunks,)),
            dma((3,)),
            dma((chunks,)),
            dma((3 * layers, chunks)),
            dma((3 * layers, chunks)),
        ],
        compiler_params=pltpu.CompilerParams(
            collective_id=0, has_side_effects=True, vmem_limit_bytes=67043328
        ),
    )(ids, tables.reshape(slots_local, peers, slot_rows // peers, share), placing, cross_down, cross_up, cross_bias)


def solution(mesh):
    return jax.shard_map(
        per_device,
        mesh=mesh,
        in_specs=(
            P("batch", None),
            P(),
            P("batch", None, None),
            P(None, "mp", None),
            P(None, None, "mp"),
            P(None, "mp"),
        ),
        out_specs=P("batch", "mp"),
        check_vma=False,
    )
```

time: 465 us -> 216 us (0.46)
  Pallas kernels: 0 us -> 203 us
  blocking collectives: 194 us -> 0 us
  local copies, waits for them, and re-layouts: 179 us -> 11.8 us
  matrix products: 42.3 us -> 0 us
  other arithmetic: 30.7 us -> 0.82 us
  waiting for transfers between devices: 12.3 us -> 0 us
    pallas_call x0 -> x1, Pallas kernels: none -> 203 us  [per_device(): pl.pallas_call(functools.partial(kernel, (groups, members, chunks, share,...]
    all_to_all x4 -> x0, blocking collectives: 194 us -> none  [the longest x1 109 us: one_exchange(): parts = lax.all_to_all(parts, axis, split_axis=0, concat_axis=0, tiled=True)]
    gather x2 -> x0, local copies, waits for them, and re-layouts: 115 us -> none  [per_device(): jnp.take(tables[slot], wanted[slot].reshape(sources * share), axis=0)]
    dot_general x5 -> x0, matrix products: 42.3 us -> none  [the longest x2 19.3 us: per_device(): jnp.dot(low, cross_up[layer], preferred_element_type=jnp.float32)]
    select_n x2, other arithmetic: 23 us -> 0.01 us  [the longest x1 0.01 us: per_device(): lane % 4]
    reshape x2 -> x1, local copies, waits for them, and re-layouts: 20.5 us -> 1.58 us  [per_device(): mine = lookup_ids.reshape(slots_local, groups, chunks, members, share)]
    select_n x2 -> x0, local copies, waits for them, and re-layouts: 13 us -> none  [per_device(): jnp.take(tables[slot], wanted[slot].reshape(sources * share), axis=0)]
    all_to_all x1 -> x0, waiting for transfers between devices: 12.3 us -> none  [from_everyone(): lax.all_to_all(jnp.broadcast_to(x[None], (size, *x.shape)), axis, 0, 0, t...]
  transfers between devices with their start and end apart: 1 -> 0, of which waited for: 1 -> 0; matrix products, arithmetic and copies ran while one was open for 3% -> 0% of each run, Pallas kernels for 0% -> 0%
where the time goes in v1:
time: 216 us; the launch traced here: 215 us
  Pallas kernels  203 us (94%)
  local copies, waits for them, and re-layouts  11.8 us (5%)
    pallas_call x1, Pallas kernels, per_device(): pl.pallas_call(functools.partial(kernel, (groups, members, chunks, share,...  203 us
    unnamed x1, local copies, waits for them, and re-layouts  8.44 us

profile of v1, /device:TPU:1, one launch (start us, length us, event | category | flops | bytes accessed | tf_op | source)
XLA Modules:
  0.0 215.2 jit_solution(5641227491404099866)
XLA Ops:
  0.0 0.7 broadcast_in_dim.2
  0.7 0.1 eq.34
  0.8 0.8 and_convert_fusion.placing
  1.7 1.6 reshape.41
  3.2 0.1 constant_dynamic-slice_fusion
  3.4 0.8 copy.7
  4.1 202.6 %shard_map.64 = bf16[2048,2048]{1,0:T(8,128)(2,1)} custom-call(s32[32768]{0:T(1024)} %bitcast.7, bf16[2,128,64,128]{3,2,1,0:T(8,128)(2,1)} %bitcast.6, bf16[256,256]{1,0:T(8,128)(2,1)} %and_convert_fusion.placing, bf16[2,2048,512]{2,1,0:T(8,128)(2,1)} %downs.1, bf16[2,512,2048]{2,1,0:T(8,128)(2,1)} %ups.1, f32[2,2048]{1,0:T(2,128)} %bias.1), custom_call_target="tpu_custom_call" | custom-call | tf_op jit(solution)/shard_map/pallas_call | solution.py:308
  206.7 8.4 %copy.9 = bf16[2048,2048]{1,0:T(8,128)(2,1)} copy(bf16[2048,2048]{1,0:T(8,128)(2,1)} %shard_map.64) | data formatting | bytes 16777216
  (2 shorter events, 0.0 us)

commit v2 on v1

--- a/solution.py
+++ b/solution.py
@@ -8,7 +8,6 @@
 from jax.sharding import PartitionSpec as P
 
 MESH = pl.DeviceIdType.MESH
-UNROLL = 64
 F32 = jnp.float32
 BF16 = jnp.bfloat16
 
@@ -23,7 +22,8 @@
     bias,
     out,
     table,
-    rows,
+    rows_a,
+    rows_b,
     pick,
     message,
     landed,
@@ -97,19 +97,18 @@
 
         lax.fori_loop(0, slot_rows // block_rows, widen, 0)
 
-    def look(chunk, dest):
-        def group(g, _):
-            for u in range(UNROLL):
-                for slot in range(2):
-                    index = ids[(dest * chunks + chunk) * (2 * share) + slot * share + g * UNROLL + u]
-                    rows[g, u : u + 1, slot * 128 : (slot + 1) * 128] = table[
-                        pl.ds(index + slot * slot_rows, 1), :
-                    ]
-            return 0
-
-        lax.fori_loop(0, share // UNROLL, group, 0)
-        looked = rows[...].reshape(share, 256).astype(BF16)
-        return (
+    def look(rows, chunk, dest):
+        first_id = (dest * chunks + chunk) * (2 * share)
+        for u in range(share):
+            for slot in range(2):
+                index = ids[first_id + slot * share + u]
+                rows[u : u + 1, slot * 128 : (slot + 1) * 128] = table[
+                    pl.ds(index + slot * slot_rows, 1), :
+                ]
+
+    def packed(rows, chunk, dest):
+        looked = rows[...].astype(BF16)
+        message[chunk, pl.ds(dest * members, members)] = (
             lax.dot_general(
                 pick[...], looked, (((1,), (1,)), ((), ())), preferred_element_type=F32
             )
@@ -127,27 +126,42 @@
             device_id_type=MESH,
         ).start()
 
-    def chunk_out(chunk, _):
-        def one(i, _):
-            dest = lax.rem(b + i, groups)
-            message[chunk, pl.ds(dest * members, members)] = look(chunk, dest)
-
-            @pl.when(jnp.logical_and(chunk == 0, i == 1))
+    def to_group(chunk, dest):
+        for k in range(members):
+            send(chunk, dest, lax.rem(m + k, members))
+
+    def chunk_out(chunk):
+        def pair(p, _):
+            left = lax.rem(b + 1 + 2 * p, groups)
+            before = lax.rem(b + 2 * p, groups)
+            right = lax.rem(b + 2 + 2 * p, groups)
+            look(rows_a, chunk, left)
+            packed(rows_b, chunk, before)
+
+            @pl.when(p > 0)
             def _():
-                pl.semaphore_wait(barrier, peers - 1)
-
-            for k in range(members):
-                send(chunk, dest, lax.rem(m + k, members))
+                to_group(chunk, before)
+
+            look(rows_b, chunk, right)
+            packed(rows_a, chunk, left)
+
+            to_group(chunk, left)
             return 0
 
-        lax.fori_loop(1, groups, one, 0)
-        message[chunk, pl.ds(b * members, members)] = look(chunk, b)
+        lax.fori_loop(0, groups // 2, pair, 0)
+        packed(rows_b, chunk, b)
         landed[chunk, me] = message[chunk, me]
         for k in range(1, members):
             send(chunk, b, lax.rem(m + k, members))
+
+    rows_b[...] = jnp.zeros_like(rows_b)
+    pl.semaphore_wait(barrier, peers - 1)
+
+    def ahead(chunk, _):
+        chunk_out(chunk)
         return 0
 
-    lax.fori_loop(0, chunks, chunk_out, 0)
+    lax.fori_loop(0, 2, ahead, 0)
     load_down.wait()
     load_up.wait()
 
@@ -196,7 +210,7 @@
         hop_low(layer, t).wait()
 
         def block(i, _):
-            at = pl.ds(pl.multiple_of(i * 128, 128), 128)
+            at = pl.ds(pl.multiple_of(i * 256, 256), 256)
             high = (
                 jnp.dot(
                     low[t, at, :], weight_up[layer], preferred_element_type=F32
@@ -208,7 +222,7 @@
             ).astype(BF16)
             return 0
 
-        lax.fori_loop(0, tile // 128, block, 0)
+        lax.fori_loop(0, tile // 256, block, 0)
 
     def place(t):
         pltpu.make_async_copy(
@@ -240,34 +254,26 @@
     def step(i, _):
         @pl.when(i >= 2)
         def _():
+            add_far(1, i - 2)
             expand(1, i - 2, state)
             store(i - 2).start()
 
         @pl.when(jnp.logical_and(i >= 1, i <= chunks))
         def _():
+            add_far(0, i - 1)
             expand(0, i - 1, emb)
             project(1, i - 1, state)
+            add_near(1, i - 1)
 
         @pl.when(i < chunks)
         def _():
             place(i)
             project(0, i, emb)
-
-        @pl.when(jnp.logical_and(i >= 1, i <= chunks))
+            add_near(0, i)
+
+        @pl.when(i + 2 < chunks)
         def _():
-            add_near(1, i - 1)
-
-        @pl.when(i < chunks)
-        def _():
-            add_near(0, i)
-
-        @pl.when(jnp.logical_and(i >= 1, i <= chunks))
-        def _():
-            add_far(1, i - 1)
-
-        @pl.when(i < chunks)
-        def _():
-            add_far(0, i)
+            chunk_out(i + 2)
 
         return 0
 
@@ -312,7 +318,8 @@
         out_specs=hbm,
         scratch_shapes=[
             pltpu.VMEM((slots_local * slot_rows, emb_dim), F32),
-            pltpu.VMEM((share // UNROLL, UNROLL, slots_local * emb_dim), F32),
+            pltpu.VMEM((share, slots_local * emb_dim), F32),
+            pltpu.VMEM((share, slots_local * emb_dim), F32),
             pltpu.VMEM((256, 256), BF16),
             pltpu.VMEM((chunks, peers, 64, share), BF16),
             pltpu.VMEM((chunks, peers, 64, share), BF16),

time: 216 us -> 198 us (0.917)
  Pallas kernels: 203 us -> 185 us
    pallas_call x1, Pallas kernels: 203 us -> 185 us  [per_device(): pl.pallas_call(functools.partial(kernel, (groups, members, chunks, share,...]
where the time goes in v2:
time: 198 us
  Pallas kernels  185 us (93%)
  local copies, waits for them, and re-layouts  11.8 us (6%)
    pallas_call x1, Pallas kernels, per_device(): pl.pallas_call(functools.partial(kernel, (groups, members, chunks, share,...  185 us
    unnamed x1, local copies, waits for them, and re-layouts  8.44 us

profile of v2, /device:TPU:1, one launch (start us, length us, event | category | flops | bytes accessed | tf_op | source)
XLA Modules:
  0.0 197.9 jit_solution(9414443382050377504)
XLA Ops:
  0.0 0.7 broadcast_in_dim.2
  0.7 0.1 eq.34
  0.8 0.8 and_convert_fusion.placing
  1.7 1.6 reshape.41
  3.2 0.1 constant_dynamic-slice_fusion
  3.4 0.8 copy.7
  4.1 185.3 %shard_map.64 = bf16[2048,2048]{1,0:T(8,128)(2,1)} custom-call(s32[32768]{0:T(1024)} %bitcast.7, bf16[2,128,64,128]{3,2,1,0:T(8,128)(2,1)} %bitcast.6, bf16[256,256]{1,0:T(8,128)(2,1)} %and_convert_fusion.placing, bf16[2,2048,512]{2,1,0:T(8,128)(2,1)} %downs.1, bf16[2,512,2048]{2,1,0:T(8,128)(2,1)} %ups.1, f32[2,2048]{1,0:T(2,128)} %bias.1), custom_call_target="tpu_custom_call" | custom-call | tf_op jit(solution)/shard_map/pallas_call | solution.py:314
  189.5 8.4 %copy.9 = bf16[2048,2048]{1,0:T(8,128)(2,1)} copy(bf16[2048,2048]{1,0:T(8,128)(2,1)} %shard_map.64) | data formatting | bytes 16777216
  (2 shorter events, 0.0 us)
